TPU v7x, 128 devices: a whole 4x4x4 slice. The times are simulated.
128 devices in a mesh: dp: 8 (over x_lo, y), expert: 16 (over z, x_hi, core).
Axes of the slice: x: 4 (x_hi: 2, x_lo: 2; x = x_hi * 2 + x_lo), y: 4, z: 4, core: 2. Of those that a mesh axis runs over, the one named last changes fastest.
Arguments:
- tokens: bfloat16 [16384, 1536], P(('dp', 'expert')), may hold values from -6 to 6
- gate_prob: float32 [16384], P(('dp', 'expert')), may hold values from 0.2 to 1
- expert_index: int32 [16384], P(('dp', 'expert')), may hold values from 0 to 31, as said below
- slot_index: int32 [16384], P(('dp', 'expert')), may hold values from 0 to 127, as said below
- dropped: int32 [16384], P(('dp', 'expert')), may hold values from 0 to 1
- cotangent: bfloat16 [16384, 1536], P(('dp', 'expert')), may hold values from -6 to 6
- expert_in: bfloat16 [32, 1536, 6144], P('expert', None, 'dp'), may hold values from -0.15625 to 0.15625
- expert_out: bfloat16 [32, 6144, 1536], P('expert', 'dp'), may hold values from -0.078125 to 0.078125
- residual_in: bfloat16 [1536, 3072], P(None, 'dp'), may hold values from -0.15625 to 0.15625
- residual_out: bfloat16 [3072, 1536], P('dp'), may hold values from -0.109375 to 0.109375
Outputs:
- output: bfloat16 [16384, 1536], P(('dp', 'expert'))
- grad_tokens: bfloat16 [16384, 1536], P(('dp', 'expert'))
- grad_gate: float32 [16384], P(('dp', 'expert'))
- grad_expert_in: bfloat16 [32, 1536, 6144], P('expert', None, 'dp')
- grad_expert_out: bfloat16 [32, 6144, 1536], P('expert', 'dp')
- grad_residual_in: bfloat16 [1536, 3072], P(None, 'dp')
- grad_residual_out: bfloat16 [3072, 1536], P('dp')
Inputs may be any that keep to these rules, and one draw needn't show every extreme that they name: `expert_index`: on every device, at least 7 tokens choose one expert, the same expert on all devices, and the tokens in its first 5 slots are not dropped. `slot_index`: on each device the tokens of one expert hold the slots 0 to n - 1 once each, n being their count; dropped tokens take the highest slots of their expert; on some device all tokens choose one expert.
All inputs are finite; a program needn't handle non-finite values.
Results may differ from a plain program's by a relative error of at most 0.018.
Values may be sent and summed in bfloat16 or wider, within the bound.
No kernel may reach another device: no remote copies, remote signals or barrier semaphores. Data moves between devices by JAX's collectives and lax.ppermute only.
A program may use at most 192 MiB of HBM per device.

v0:
```python
import jax
import jax.numpy as jnp
from jax import lax
from jax.sharding import Mesh
from jax.sharding import PartitionSpec as P

EXPERT = ("expert_0", "expert_1", "expert_2")
DP_EXPERT = ("dp", "expert_0", "expert_1", "expert_2")


def in_blocks(value, dim, peers):
    before, after = (value.shape[:dim], value.shape[dim + 1 :])
    return jnp.moveaxis(value.reshape(*before, peers, -1, *after), dim, 0)


def in_order(blocks, dim):
    lengths = list(blocks.shape[1:])
    lengths[dim] *= blocks.shape[0]
    return jnp.moveaxis(blocks, 0, dim).reshape(lengths)


def exchange_in_order(blocks, axes, turns):
    inside = blocks.shape[1:]
    whole = blocks.reshape(*(lax.axis_size(a) for a in axes), *inside)
    for k in turns:
        whole = lax.all_to_all(whole, axes[k], k, k, tiled=True)
    return whole.reshape(-1, *inside)


def exchange_by_chip(value, groups, turns, split_dim, concat_dim):
    peers = lax.axis_size(groups[0]) * lax.axis_size(groups[1])
    blocks = in_blocks(value, split_dim, peers)
    return in_order(exchange_in_order(blocks, groups, turns), concat_dim)


def sum_packed(arrays, axis, dims):
    peers = lax.axis_size(axis)
    blocks = [in_blocks(a, dim, peers) for a, dim in zip(arrays, dims)]
    lines = jnp.concatenate([b.reshape(peers, -1) for b in blocks], axis=1)
    rows = max(16, -(-lines.shape[1] // 1024) * 8)
    lines = jnp.pad(lines, ((0, 0), (0, rows * 128 - lines.shape[1]))).reshape(-1, 128)
    flat, at, gathered = (lax.psum_scatter(lines, axis, tiled=True).reshape(-1), 0, [])
    for b in blocks:
        part = b[0]
        gathered.append(flat[at : at + part.size].reshape(part.shape))
        at += part.size
    return tuple(gathered)


def in_one(arrays, axis):
    flat, at, gathered = (jnp.concatenate([a.reshape(-1) for a in arrays]), 0, [])
    running = lax.psum(flat, axis)
    for a in arrays:
        gathered.append(running[at : at + a.size].reshape(a.shape))
        at += a.size
    return tuple(gathered)


def gelu_tanh(values):
    return jax.nn.gelu(values, approximate=True)


def place_rows(values, position, slot_count):
    buffer = jnp.zeros((slot_count + 1, values.shape[1]), values.dtype)
    return buffer.at[position].set(values)[:slot_count]


def fetch_rows(buffer, position):
    padded = jnp.concatenate([buffer, jnp.zeros((1, buffer.shape[1]), buffer.dtype)], axis=0)
    return padded[position]


def on_device(
    tokens,
    gate_prob,
    expert_index,
    slot_index,
    dropped,
    cotangent,
    expert_in,
    expert_out,
    residual_in,
    residual_out,
):
    groups = lax.axis_size("dp")
    host_count = lax.axis_size(EXPERT)
    local_count = expert_in.shape[0]
    experts_all = local_count * host_count
    row_count, model_width = tokens.shape
    capacity = max(2, 5 * row_count // (4 * experts_all))
    kept = (dropped == 0) & (slot_index < capacity)
    kept_float = kept.astype(jnp.float32)
    gate_kept = gate_prob * kept_float
    own_slots = experts_all * capacity
    own_index = jnp.where(kept, expert_index * capacity + slot_index, -1)
    own_position = jnp.where(kept, own_index, own_slots)

    def to_column(row_values, row_scale):
        values = (row_values.astype(jnp.float32) * row_scale[:, None]).astype(jnp.bfloat16)
        own_buffer = place_rows(values, own_position, own_slots).reshape(
            host_count, local_count, capacity, model_width
        )
        arrived = exchange_by_chip(own_buffer, (("expert_0", "expert_1"), "expert_2"), (1, 0), 0, 0)
        col_rows, column = (
            lax.all_gather(row_values, "dp", axis=0, tiled=True),
            lax.all_gather(arrived[None], "dp", axis=0, tiled=True),
        )
        return (col_rows, column)

    def from_column(dense_part, expert_part):
        dense_sum, expert_sum = tuple(
            (
                part.astype(jnp.float32)
                for part in sum_packed(
                    (dense_part.astype(jnp.bfloat16), expert_part.astype(jnp.bfloat16)),
                    "dp",
                    (0, 0),
                )
            )
        )
        own_result = lax.all_to_all(
            expert_sum[0].astype(jnp.bfloat16), EXPERT, split_axis=0, concat_axis=0, tiled=True
        )
        return (dense_sum[0], own_result.reshape(own_slots, model_width))

    unit_scale = jnp.ones_like(gate_prob)
    col_tokens, column = to_column(tokens, unit_scale)
    pre_expert = jnp.einsum(
        "abjcd,jdf->abjcf", column, expert_in, preferred_element_type=jnp.float32
    )
    hidden_f, expert_back = jax.vjp(gelu_tanh, pre_expert)
    hidden = hidden_f.astype(jnp.bfloat16)
    expert_part = jnp.einsum(
        "abjcf,jfd->abjcd", hidden, expert_out, preferred_element_type=jnp.float32
    )
    pre_dense = jnp.dot(col_tokens, residual_in, preferred_element_type=jnp.float32)
    dense_f, dense_back = jax.vjp(gelu_tanh, pre_dense)
    dense_hidden = dense_f.astype(jnp.bfloat16)
    dense_part = jnp.dot(dense_hidden, residual_out, preferred_element_type=jnp.float32).reshape(
        groups, row_count, model_width
    )
    dense_sum, expert_rows = from_column(dense_part, expert_part)
    expert_token = fetch_rows(expert_rows, own_position).astype(jnp.float32)
    output = (dense_sum + gate_kept[:, None] * expert_token).astype(jnp.bfloat16)
    grad_gate = kept_float * jnp.sum(cotangent.astype(jnp.float32) * expert_token, axis=1)
    col_cotangent, grad_column = to_column(cotangent, gate_kept)
    grad_hidden = jnp.einsum(
        "abjcd,jfd->abjcf", grad_column, expert_out, preferred_element_type=jnp.float32
    )
    grad_pre = expert_back(grad_hidden)[0].astype(jnp.bfloat16)
    grad_expert_out = jnp.einsum(
        "abjcf,abjcd->jfd", hidden, grad_column, preferred_element_type=jnp.float32
    ).astype(jnp.bfloat16)
    grad_expert_in = jnp.einsum(
        "abjcd,abjcf->jdf", column, grad_pre, preferred_element_type=jnp.float32
    ).astype(jnp.bfloat16)
    expert_dx = jnp.einsum(
        "abjcf,jdf->abjcd", grad_pre, expert_in, preferred_element_type=jnp.float32
    )
    dense_grad_hidden = jnp.einsum(
        "td,fd->tf", col_cotangent, residual_out, preferred_element_type=jnp.float32
    )
    dense_grad_pre = dense_back(dense_grad_hidden)[0].astype(jnp.bfloat16)
    out_partial = jnp.einsum(
        "tf,td->fd", dense_hidden, col_cotangent, preferred_element_type=jnp.float32
    )
    in_partial = jnp.einsum(
        "td,tf->df", col_tokens, dense_grad_pre, preferred_element_type=jnp.float32
    )
    in_total, out_total = tuple(
        (
            part.astype(jnp.float32)
            for part in in_one(
                (in_partial.astype(jnp.bfloat16), out_partial.astype(jnp.bfloat16)), EXPERT
            )
        )
    )
    dense_dx = jnp.einsum(
        "tf,df->td", dense_grad_pre, residual_in, preferred_element_type=jnp.float32
    ).reshape(groups, row_count, model_width)
    dense_dx_sum, expert_dx_rows = from_column(dense_dx, expert_dx)
    grad_tokens = (
        dense_dx_sum + fetch_rows(expert_dx_rows, own_position).astype(jnp.float32)
    ).astype(jnp.bfloat16)
    return (
        output,
        grad_tokens,
        grad_gate,
        grad_expert_in,
        grad_expert_out,
        in_total.astype(jnp.bfloat16),
        out_total.astype(jnp.bfloat16),
    )


def solution(mesh):
    finer = Mesh(
        mesh.devices.reshape(mesh.shape["dp"], 4, 2, 2), ("dp", "expert_0", "expert_1", "expert_2")
    )
    in_specs = (
        P(DP_EXPERT, None),
        P(DP_EXPERT),
        P(DP_EXPERT),
        P(DP_EXPERT),
        P(DP_EXPERT),
        P(DP_EXPERT, None),
        P(EXPERT, None, "dp"),
        P(EXPERT, "dp", None),
        P(None, "dp"),
        P("dp", None),
    )
    out_specs = (
        P(DP_EXPERT, None),
        P(DP_EXPERT, None),
        P(DP_EXPERT),
        P(EXPERT, None, "dp"),
        P(EXPERT, "dp", None),
        P(None, "dp"),
        P("dp", None),
    )
    return jax.shard_map(
        on_device, mesh=finer, in_specs=in_specs, out_specs=out_specs, check_vma=False
    )
```

profile of v0, /device:TPU:1, one launch (start us, length us, event | category | flops | bytes accessed | tf_op | source)
XLA Modules:
  0.0 565.7 jit_solution(12791289579129211362)
XLA Ops:
  17.4 21.9 %all_to_all.31 = bf16[8,2,1,2,5,1536]{5,3,4,2,1,0:T(2,128)(2,1)S(1)} all-to-all(bf16[8,2,1,2,5,1536]{5,3,4,2,1,0:T(2,128)(2,1)S(1)} %copy.23), channel_id=1, replica_groups=mesh['dp'=8,'expert_0'=4,'expert_1'=2,'expert_2'=2] {'expert_0','expert_1'}, dimensions={0} | all-to-all | bytes 983040 | tf_op jit(solution)/shard_map/all_to_all | solution.py:26
  42.7 6.4 %all_to_all.32 = bf16[8,2,1,2,5,1536]{5,0,4,3,2,1:T(8,128)(2,1)S(1)} all-to-all(bf16[8,2,1,2,5,1536]{5,0,4,3,2,1:T(8,128)(2,1)S(1)} %copy.28), channel_id=1, replica_groups=mesh['dp'=8,'expert_0'=4,'expert_1'=2,'expert_2'=2] {'expert_2'}, dimensions={1} | all-to-all | bytes 983040 | tf_op jit(solution)/shard_map/all_to_all | solution.py:26
  54.4 14.5 %all-to-all-done.4 = bf16[8,2,1,2,5,1536]{5,3,4,2,1,0:T(2,128)(2,1)S(1)} async-done(((bf16[8,2,1,2,5,1536]{5,3,4,2,1,0:T(2,128)(2,1)}), bf16[8,2,1,2,5,1536]{5,3,4,2,1,0:T(2,128)(2,1)S(1)}, u32[]{:S(2)}, u32[]{:S(2)}) %all-to-all-start.4) | async-done | bytes 491552 | tf_op jit(solution)/shard_map/all_to_all | solution.py:26
  74.9 33.2 %all-gather.5.cloned.1.call-done = bf16[1024,1536]{1,0:T(8,128)(2,1)} async-done(((bf16[128,1536]{1,0:T(8,128)(2,1)}), bf16[1024,1536]{1,0:T(8,128)(2,1)}) %all-gather.5.cloned.1.call-update) | async-done | bytes 3145744 | tf_op jit(solution)/shard_map/all_gather | solution.py:105
  108.1 6.1 %fusion.44 = (bf16[1024,384]{1,0:T(8,128)(2,1)S(1)}, f32[1024,384]{1,0:T(8,128)}) fusion(f32[1024,384]{1,0:T(8,128)} %fusion.56, bf16[1024,1536]{1,0:T(8,128)(2,1)} %all-gather.5.cloned.1.call-done, bf16[1536,384]{1,0:T(8,128)(2,1)S(1)} %copy-done), kind=kOutput, calls=%fused_computation.54 | convolution fusion | flops 1215823872 | bytes 8257536 | tf_op jit(solution)/shard_map/dot_general | solution.py:136
  125.4 9.5 %pad_maximum_fusion.2 = bf16[1179648]{0:T(1024)(128)(2,1)} fusion(bf16[589824]{0:T(1024)(128)(2,1)S(1)} %reshape.102, bf16[589824]{0:T(1024)(128)(2,1)S(1)} %reshape.101), kind=kLoop, calls=%fused_computation.43 | loop fusion | flops 4718592 | bytes 4718592 | tf_op jit(solution)/shard_map/concatenate | solution.py:51
  153.3 8.6 %all-gather.7.cloned.1.call-done = bf16[8,16,2,5,1536]{4,1,3,0,2:T(8,128)(2,1)} async-done(((bf16[1,16,2,5,1536]{4,1,3,0,2:T(8,128)(2,1)}), bf16[8,16,2,5,1536]{4,1,3,0,2:T(8,128)(2,1)}) %all-gather.7.cloned.1.call-update) | async-done | bytes 3932176 | tf_op jit(solution)/shard_map/all_gather | solution.py:106
  161.8 9.1 %fusion.24 = (bf16[8,16,2,5,768]{4,1,3,0,2:T(8,128)(2,1)S(1)}, f32[2,8,16,5,768]{4,2,3,1,0:T(8,128)}) fusion(bf16[8,16,2,5,1536]{4,1,3,0,2:T(8,128)(2,1)} %all-gather.7.cloned.1.call-done, bf16[2,1536,768]{2,1,0:T(8,128)(2,1)} %param.16), kind=kOutput, calls=%fused_computation.33 | convolution fusion | flops 3028746240 | bytes 14548992 | tf_op jit(solution)/shard_map/abjcd,jdf->abjcf/dot_general | solution.py:128
  172.2 6.2 %fusion.30 = bf16[8,16,2,5,1536]{4,1,3,0,2:T(8,128)(2,1)S(1)} fusion(bf16[8,16,2,5,768]{4,1,3,0,2:T(8,128)(2,1)S(1)} %get-tuple-element.11, bf16[2,768,1536]{2,1,0:T(8,128)(2,1)} %param.17), kind=kOutput, calls=%fused_computation.39 | convolution fusion | flops 3021864960 | bytes 10616832 | tf_op jit(solution)/shard_map/abjcf,jfd->abjcd/dot_general | solution.py:133
  183.7 10.9 %reshape_reshape.8 = bf16[8,245760]{1,0:T(8,128)(2,1)} reshape(bf16[8,16,2,5,1536]{4,3,2,1,0:T(8,128)(2,1)} %copy.25) | data formatting | bytes 7864320 | tf_op jit(solution)/shard_map/reshape;reshape | solution.py:39
  194.5 8.5 %pad_maximum_fusion = bf16[8,442368]{1,0:T(8,128)(2,1)} fusion(bf16[8,245760]{1,0:T(8,128)(2,1)} %reshape_reshape.8, bf16[8,196608]{1,0:T(8,128)(2,1)} %convert_element_type.109), kind=kLoop, calls=%fused_computation.6 | loop fusion | flops 14155776 | bytes 14155776 | tf_op jit(solution)/shard_map/concatenate | solution.py:39
  203.0 9.2 %reshape.95 = bf16[27648,128]{1,0:T(8,128)(2,1)} reshape(bf16[8,442368]{1,0:T(8,128)(2,1)} %pad_maximum_fusion) | data formatting | bytes 14155776 | tf_op jit(solution)/shard_map/reshape | solution.py:41
  212.5 9.9 %fusion.20 = bf16[8,16,2,5,768]{4,1,3,0,2:T(8,128)(2,1)S(1)} fusion(f32[2,8,16,5,768]{4,2,3,1,0:T(8,128)} %get-tuple-element.12, bf16[8,16,2,5,1536]{4,1,3,0,2:T(8,128)(2,1)} %all-gather.11.cloned.1.call-done, bf16[2,768,1536]{2,1,0:T(8,128)(2,1)} %param.17), kind=kOutput, calls=%fused_computation.26 | convolution fusion | flops 3039559680 | bytes 14548992 | tf_op jit(solution)/shard_map/abjcd,jfd->abjcf/dot_general | solution.py:147
  226.2 5.3 copy.31
  231.5 10.8 %reshape_reshape.9 = bf16[8,245760]{1,0:T(8,128)(2,1)} reshape(bf16[8,16,2,5,1536]{4,3,2,1,0:T(8,128)(2,1)} %copy.31) | data formatting | bytes 7864320 | tf_op jit(solution)/shard_map/reshape;reshape | solution.py:39
  242.3 8.6 %pad_maximum_fusion.1 = bf16[8,442368]{1,0:T(8,128)(2,1)} fusion(bf16[8,245760]{1,0:T(8,128)(2,1)} %reshape_reshape.9, bf16[8,196608]{1,0:T(8,128)(2,1)} %convert_element_type.119), kind=kLoop, calls=%fused_computation.7 | loop fusion | flops 14155776 | bytes 14155776 | tf_op jit(solution)/shard_map/concatenate | solution.py:39
  250.9 9.1 %reshape.98 = bf16[27648,128]{1,0:T(8,128)(2,1)} reshape(bf16[8,442368]{1,0:T(8,128)(2,1)} %pad_maximum_fusion.1) | data formatting | bytes 14155776 | tf_op jit(solution)/shard_map/reshape | solution.py:41
  261.6 7.8 %bitcast_convert_fusion = bf16[2,768,1536]{2,1,0:T(8,128)(2,1)} fusion(bf16[8,16,2,5,1536]{4,1,3,0,2:T(8,128)(2,1)} %all-gather.11.cloned.1.call-done, bf16[8,16,2,5,768]{4,1,3,0,2:T(8,128)(2,1)S(1)} %copy-done.19), kind=kOutput, calls=%fused_computation.4 | convolution fusion | flops 3022258176 | bytes 10616832 | tf_op jit(solution)/shard_map/abjcf,abjcd->jfd/dot_general | solution.py:151
  269.4 5.6 bitcast_convert_fusion.1
  275.0 85.9 %all-reduce.4.cloned.1.call-done = bf16[1179648]{0:T(1024)(128)(2,1)} async-done(((bf16[1179648]{0:T(1024)(128)(2,1)}), bf16[1179648]{0:T(1024)(128)(2,1)}) %all-reduce.4.cloned.1.call-update) | async-done | bytes 2359312 | tf_op jit(solution)/shard_map/psum | solution.py:52
  366.2 78.5 %reduce-scatter.3.cloned.1.call-done = bf16[3456,128]{1,0:T(8,128)(2,1)} async-done(((bf16[27648,128]{1,0:T(8,128)(2,1)}), bf16[3456,128]{1,0:T(8,128)(2,1)}) %reduce-scatter.3.cloned.1.call-update) | async-done | bytes 884752 | tf_op jit(solution)/shard_map/reduce_scatter | solution.py:42
  447.7 7.7 %all-to-all-start.2 = ((bf16[16,2,5,1536]{3,1,2,0:T(2,128)(2,1)}), bf16[16,2,5,1536]{3,1,2,0:T(2,128)(2,1)S(1)}, u32[]{:S(2)}, u32[]{:S(2)}) async-start(bf16[16,2,5,1536]{3,1,2,0:T(2,128)(2,1)} %copy.26), calls=%async_computation.3 | async-start | bytes 983040 | tf_op jit(solution)/shard_map/all_to_all | solution.py:121
  455.4 74.2 %reduce-scatter.5.cloned.1.call-done = bf16[3456,128]{1,0:T(8,128)(2,1)} async-done(((bf16[27648,128]{1,0:T(8,128)(2,1)}), bf16[3456,128]{1,0:T(8,128)(2,1)}) %reduce-scatter.5.cloned.1.call-update) | async-done | bytes 884752 | tf_op jit(solution)/shard_map/reduce_scatter | solution.py:42
  536.2 7.9 %all-to-all-start.5 = ((bf16[16,2,5,1536]{3,1,2,0:T(2,128)(2,1)}), bf16[16,2,5,1536]{3,1,2,0:T(2,128)(2,1)}, u32[]{:S(2)}, u32[]{:S(2)}) async-start(bf16[16,2,5,1536]{3,1,2,0:T(2,128)(2,1)} %copy.32), calls=%async_computation.7 | async-start | bytes 983040 | tf_op jit(solution)/shard_map/all_to_all | solution.py:121
  (121 shorter events, 95.4 us)
Async XLA Ops:
  7.2 100.9 %copy-start = (bf16[1536,384]{1,0:T(8,128)(2,1)S(1)}, bf16[1536,384]{1,0:T(8,128)(2,1)}, u32[]{:S(2)}) copy-start(bf16[1536,384]{1,0:T(8,128)(2,1)} %param.18) | copy-start | bytes 3538948
  7.2 62.9 %all-gather.9.cloned.1.call-start = ((), (), s32[]{:S(2)}) async-start(), calls=%async_computation.11 | async-start | bytes 3538944 | tf_op jit(solution)/shard_map/all_gather | solution.py:105
  7.9 100.2 %all-gather.5.cloned.1.call-start = ((), (), s32[]{:S(2)}) async-start(), calls=%async_computation.8 | async-start | bytes 3538944 | tf_op jit(solution)/shard_map/all_gather | solution.py:105
  8.7 153.2 %all-gather.7.cloned.1.call-start = ((), (), s32[]{:S(2)}) async-start(), calls=%async_computation.9 | async-start | bytes 4423680 | tf_op jit(solution)/shard_map/all_gather | solution.py:106
  11.5 28.6 %copy-start.7 = (s32[128]{0:T(128)S(1)}, s32[128]{0:T(128)}, u32[]{:S(2)}) copy-start(s32[128]{0:T(128)} %param.13) | copy-start | bytes 1540
  11.5 28.6 %copy-start.9 = (s32[128]{0:T(128)S(1)}, s32[128]{0:T(128)}, u32[]{:S(2)}) copy-start(s32[128]{0:T(128)} %param.14) | copy-start | bytes 1540
  11.5 28.6 %copy-start.11 = (f32[128]{0:T(128)S(1)}, f32[128]{0:T(128)}, u32[]{:S(2)}) copy-start(f32[128]{0:T(128)} %param.11) | copy-start | bytes 1540
  11.5 29.2 %copy-start.2 = (bf16[128,1536]{1,0:T(8,128)(2,1)S(1)}, bf16[128,1536]{1,0:T(8,128)(2,1)}, u32[]{:S(2)}) copy-start(bf16[128,1536]{1,0:T(8,128)(2,1)} %param.15) | copy-start | bytes 1179652
  42.7 27.4 %copy-start.14 = (bf16[384,1536]{1,0:T(8,128)(2,1)S(1)}, bf16[384,1536]{1,0:T(8,128)(2,1)}, u32[]{:S(2)}) copy-start(bf16[384,1536]{1,0:T(8,128)(2,1)} %param.19) | copy-start | bytes 3538948
  50.2 18.7 %all-to-all-start.4 = ((bf16[8,2,1,2,5,1536]{5,3,4,2,1,0:T(2,128)(2,1)}), bf16[8,2,1,2,5,1536]{5,3,4,2,1,0:T(2,128)(2,1)S(1)}, u32[]{:S(2)}, u32[]{:S(2)}) async-start(bf16[8,2,1,2,5,1536]{5,3,4,2,1,0:T(2,128)(2,1)} %copy.29), calls=%async_computation.5 | async-start | bytes 983040 | tf_op jit(solution)/shard_map/all_to_all | solution.py:26
  53.7 158.8 %all-gather.11.cloned.1.call-start = ((), (), s32[]{:S(2)}) async-start(), calls=%async_computation.12 | async-start | bytes 4423680 | tf_op jit(solution)/shard_map/all_gather | solution.py:106
  69.8 291.1 %all-reduce.4.cloned.1.call-start = ((), (), s32[]{:S(2)}) async-start(), calls=%async_computation.14 | async-start | bytes 4718592 | tf_op jit(solution)/shard_map/psum | solution.py:52
  108.1 7.0 %copy-start.13 = (bf16[1024,1536]{1,0:T(8,128)(2,1)S(1)}, bf16[1024,1536]{1,0:T(8,128)(2,1)}, u32[]{:S(2)}) copy-start(bf16[1024,1536]{1,0:T(8,128)(2,1)} %all-gather.5.cloned.1.call-done) | copy-start | bytes 9437188
  139.6 5.1 copy-start.15
  139.6 5.1 copy-start.17
  153.2 291.5 %reduce-scatter.3.cloned.1.call-start = ((), (), s32[]{:S(2)}) async-start(), calls=%async_computation.10 | async-start | bytes 7962624 | tf_op jit(solution)/shard_map/reduce_scatter | solution.py:42
  203.0 19.4 %slice-start.1 = ((s8[4718592]{0:T(1024)(128)(4,1)}), s8[524288]{0:T(1024)(128)(4,1)S(1)}, s32[]{:S(2)}) async-start(s8[4718592]{0:T(1024)(128)(4,1)} %bitcast.86), calls=%async_computation.16 | async-start | bytes 1048576
  212.5 9.9 %slice-start.2 = ((s8[4718592]{0:T(1024)(128)(4,1)}), s8[4194304]{0:T(1024)(128)(4,1)S(1)}, s32[]{:S(2)}) async-start(s8[4718592]{0:T(1024)(128)(4,1)} %bitcast.86), calls=%async_computation.17 | async-start | bytes 8388608
  222.4 3.7 copy-start.20
  242.3 287.3 %reduce-scatter.5.cloned.1.call-start = ((), (), s32[]{:S(2)}) async-start(), calls=%async_computation.13 | async-start | bytes 7962624 | tf_op jit(solution)/shard_map/reduce_scatter | solution.py:42
  261.6 7.8 %copy-start.12 = (bf16[8,16,2,5,1536]{4,1,3,0,2:T(8,128)(2,1)S(1)}, bf16[8,16,2,5,1536]{4,1,3,0,2:T(8,128)(2,1)}, u32[]{:S(2)}) copy-start(bf16[8,16,2,5,1536]{4,1,3,0,2:T(8,128)(2,1)} %all-gather.7.cloned.1.call-done) | copy-start | bytes 11796484
  261.6 7.8 %copy-start.21 = (bf16[8,16,2,5,768]{4,1,3,0,2:T(8,128)(2,1)S(1)}, bf16[8,16,2,5,768]{4,1,3,0,2:T(8,128)(2,1)}, u32[]{:S(2)}) copy-start(bf16[8,16,2,5,768]{4,1,3,0,2:T(8,128)(2,1)} %copy-done.20) | copy-start | bytes 5898244
  447.7 87.7 %all-to-all-start.2 = ((bf16[16,2,5,1536]{3,1,2,0:T(2,128)(2,1)}), bf16[16,2,5,1536]{3,1,2,0:T(2,128)(2,1)S(1)}, u32[]{:S(2)}, u32[]{:S(2)}) async-start(bf16[16,2,5,1536]{3,1,2,0:T(2,128)(2,1)} %copy.26), calls=%async_computation.3 | async-start | bytes 983040 | tf_op jit(solution)/shard_map/all_to_all | solution.py:121
  536.2 18.8 %all-to-all-start.5 = ((bf16[16,2,5,1536]{3,1,2,0:T(2,128)(2,1)}), bf16[16,2,5,1536]{3,1,2,0:T(2,128)(2,1)}, u32[]{:S(2)}, u32[]{:S(2)}) async-start(bf16[16,2,5,1536]{3,1,2,0:T(2,128)(2,1)} %copy.32), calls=%async_computation.7 | async-start | bytes 983040 | tf_op jit(solution)/shard_map/all_to_all | solution.py:121
  (11 other events, 20.9 us)
Sparse Core Ops, SparseCore 0:
  9.6 50.7 all-gather.8
  62.1 45.9 all-gather.4
  109.8 52.0 all-gather.6
  163.3 49.1 all-gather.10
  214.8 146.0 all-reduce.3
  363.2 81.4 reduce-scatter.2
  447.1 82.4 reduce-scatter.4
where the time goes:
time: 571 us; the launch traced here: 566 us
  waiting for transfers between devices  302 us (53%)
  local copies, waits for them, and re-layouts  94.5 us (17%)
  matrix products  67.7 us (12%)
  other arithmetic  33.7 us (6%)
  blocking collectives  33.4 us (6%)
  starting transfers between devices  19.5 us (3%)
  between operations  15.1 us (3%)
    reduce_scatter x2, waiting for transfers between devices, sum_packed(): lax.psum_scatter(lines, axis, tiled=True).reshape(-1)  153 us
    psum x1, waiting for transfers between devices, in_one(): running = lax.psum(flat, axis)  85.9 us
    all_to_all x3, blocking collectives, exchange_in_order(): whole = lax.all_to_all(whole, axes[k], k, k, tiled=True)  33.4 us
    all_gather x2, waiting for transfers between devices, to_column(): lax.all_gather(row_values, 'dp', axis=0, tiled=True)  33.2 us
    another operation x2, local copies, waits for them, and re-layouts, sum_packed(): lines = jnp.concatenate([b.reshape(peers, -1) for b in blocks], axis=1)  21.7 us
    reshape x2, local copies, waits for them, and re-layouts, sum_packed(): jnp.pad(lines, ((0, 0), (0, rows * 128 - lines.shape[1]))).reshape(-1, 128)  18.3 us
    concatenate x2, other arithmetic, sum_packed(): lines = jnp.concatenate([b.reshape(peers, -1) for b in blocks], axis=1)  17 us
    all_to_all x2, starting transfers between devices, from_column(): lax.all_to_all(expert_sum[0].astype(jnp.bfloat16), EXPERT, split_axis=0,...  15.5 us
  transfers between devices with their start and end apart: 10, of which 8 were waited for; matrix products, arithmetic and copies ran while one was open for 33% of the time, Pallas kernels for 0%

commit v1 on v0

--- a/solution.py
+++ b/solution.py
@@ -6,6 +6,11 @@
 
 EXPERT = ("expert_0", "expert_1", "expert_2")
 DP_EXPERT = ("dp", "expert_0", "expert_1", "expert_2")
+
+
+def swapped_in(x, axis, dim):
+    stack = jnp.stack([x] * lax.axis_size(axis))
+    return jnp.concatenate(lax.all_to_all(stack, axis, 0, 0), axis=dim)
 
 
 def in_blocks(value, dim, peers):
@@ -102,7 +107,7 @@
         )
         arrived = exchange_by_chip(own_buffer, (("expert_0", "expert_1"), "expert_2"), (1, 0), 0, 0)
         col_rows, column = (
-            lax.all_gather(row_values, "dp", axis=0, tiled=True),
+            swapped_in(row_values, "dp", 0),
             lax.all_gather(arrived[None], "dp", axis=0, tiled=True),
         )
         return (col_rows, column)

time: 571 us -> 531 us (0.930)
  waiting for transfers between devices: 302 us -> 183 us
  blocking collectives: 33.4 us -> 107 us
    reduce_scatter x2, waiting for transfers between devices: 153 us -> 24.1 us  [sum_packed(): lax.psum_scatter(lines, axis, tiled=True).reshape(-1)]
    all_to_all x0 -> x1, blocking collectives: none -> 59.4 us  [swapped_in(): return jnp.concatenate(lax.all_to_all(stack, axis, 0, 0), axis=dim)]
    all_gather x2 -> x0, waiting for transfers between devices: 33.2 us -> none  [to_column(): lax.all_gather(row_values, 'dp', axis=0, tiled=True)]
    all_to_all x1, waiting for transfers between devices: 14.5 us -> 44.6 us  [swapped_in(): return jnp.concatenate(lax.all_to_all(stack, axis, 0, 0), axis=dim)]
    psum x1, waiting for transfers between devices: 85.9 us -> 109 us  [in_one(): running = lax.psum(flat, axis)]
    all_to_all x3 -> x4, blocking collectives: 33.4 us -> 47.8 us  [exchange_in_order(): whole = lax.all_to_all(whole, axes[k], k, k, tiled=True)]
    all_gather x2, waiting for transfers between devices: 8.86 us -> 0.02 us  [to_column(): lax.all_gather(arrived[None], 'dp', axis=0, tiled=True)]
  transfers between devices with their start and end apart: 10 -> 8, of which waited for: 8 -> 4; matrix products, arithmetic and copies ran while one was open for 33% -> 35% of each run, Pallas kernels for 0% -> 0%
where the time goes in v1:
time: 531 us; the launch traced here: 522 us
  waiting for transfers between devices  183 us (34%)
  blocking collectives  107 us (20%)
  local copies, waits for them, and re-layouts  93.2 us (18%)
  matrix products  65.9 us (12%)
  other arithmetic  33.7 us (6%)
  starting transfers between devices  22.7 us (4%)
  between operations  16.2 us (3%)
    psum x1, waiting for transfers between devices, in_one(): running = lax.psum(flat, axis)  109 us
    all_to_all x1, blocking collectives, swapped_in(): return jnp.concatenate(lax.all_to_all(stack, axis, 0, 0), axis=dim)  59.4 us
    all_to_all x4, blocking collectives, exchange_in_order(): whole = lax.all_to_all(whole, axes[k], k, k, tiled=True)  47.8 us
    all_to_all x1, waiting for transfers between devices, swapped_in(): return jnp.concatenate(lax.all_to_all(stack, axis, 0, 0), axis=dim)  44.6 us
    reduce_scatter x2, waiting for transfers between devices, sum_packed(): lax.psum_scatter(lines, axis, tiled=True).reshape(-1)  24.1 us
    another operation x2, local copies, waits for them, and re-layouts, sum_packed(): lines = jnp.concatenate([b.reshape(peers, -1) for b in blocks], axis=1)  21.6 us
    reshape x2, local copies, waits for them, and re-layouts, sum_packed(): jnp.pad(lines, ((0, 0), (0, rows * 128 - lines.shape[1]))).reshape(-1, 128)  18.4 us
    all_to_all x2, starting transfers between devices, from_column(): lax.all_to_all(expert_sum[0].astype(jnp.bfloat16), EXPERT, split_axis=0,...  17.8 us
  transfers between devices with their start and end apart: 8, of which 4 were waited for; matrix products, arithmetic and copies ran while one was open for 35% of the time, Pallas kernels for 0%

profile of v1, /device:TPU:1, one launch (start us, length us, event | category | flops | bytes accessed | tf_op | source)
XLA Modules:
  0.0 522.2 jit_solution(16390946013694561932)
XLA Ops:
  16.8 17.9 %all_to_all.41 = bf16[8,2,1,2,5,1536]{5,3,4,2,1,0:T(2,128)(2,1)S(1)} all-to-all(bf16[8,2,1,2,5,1536]{5,3,4,2,1,0:T(2,128)(2,1)S(1)} %copy.23), channel_id=1, replica_groups=mesh['dp'=8,'expert_0'=4,'expert_1'=2,'expert_2'=2] {'expert_0','expert_1'}, dimensions={0} | all-to-all | bytes 983040 | tf_op jit(solution)/shard_map/all_to_all | solution.py:31
  37.6 5.5 %all_to_all.42 = bf16[8,2,1,2,5,1536]{5,0,4,3,2,1:T(8,128)(2,1)S(1)} all-to-all(bf16[8,2,1,2,5,1536]{5,0,4,3,2,1:T(8,128)(2,1)S(1)} %copy.28), channel_id=1, replica_groups=mesh['dp'=8,'expert_0'=4,'expert_1'=2,'expert_2'=2] {'expert_2'}, dimensions={1} | all-to-all | bytes 983040 | tf_op jit(solution)/shard_map/all_to_all | solution.py:31
  43.4 19.3 %all_to_all.43 = bf16[8,2,1,2,5,1536]{5,3,4,2,1,0:T(2,128)(2,1)S(1)} all-to-all(bf16[8,2,1,2,5,1536]{5,3,4,2,1,0:T(2,128)(2,1)S(1)} %copy.29), channel_id=1, replica_groups=mesh['dp'=8,'expert_0'=4,'expert_1'=2,'expert_2'=2] {'expert_0','expert_1'}, dimensions={0} | all-to-all | bytes 983040 | tf_op jit(solution)/shard_map/all_to_all | solution.py:31
  63.0 59.4 %all_to_all.44 = bf16[8,128,1536]{2,1,0:T(8,128)(2,1)} all-to-all(bf16[8,128,1536]{2,1,0:T(8,128)(2,1)S(1)} %stack.5), channel_id=1, replica_groups=mesh['dp'=8,'expert_0'=4,'expert_1'=2,'expert_2'=2] {'dp'}, dimensions={0} | all-to-all | bytes 6291456 | tf_op jit(solution)/shard_map/all_to_all | solution.py:13
  134.4 44.6 %all-to-all-done = bf16[8,128,1536]{2,1,0:T(8,128)(2,1)} async-done(((bf16[8,128,1536]{2,1,0:T(8,128)(2,1)}), bf16[8,128,1536]{2,1,0:T(8,128)(2,1)}, u32[]{:S(2)}, u32[]{:S(2)}) %all-to-all-start) | async-done | bytes 3145760 | tf_op jit(solution)/shard_map/all_to_all | solution.py:13
  193.8 9.3 %pad_maximum_fusion.2 = bf16[1179648]{0:T(1024)(128)(2,1)} fusion(bf16[589824]{0:T(1024)(128)(2,1)S(1)} %reshape.114, bf16[589824]{0:T(1024)(128)(2,1)S(1)} %reshape.113), kind=kLoop, calls=%fused_computation.43 | loop fusion | flops 4718592 | bytes 4718592 | tf_op jit(solution)/shard_map/concatenate | solution.py:56
  221.6 9.1 %fusion.24 = (bf16[8,16,2,5,768]{4,1,3,0,2:T(8,128)(2,1)S(1)}, f32[2,8,16,5,768]{4,2,3,1,0:T(8,128)}) fusion(bf16[8,16,2,5,1536]{4,1,3,0,2:T(8,128)(2,1)} %all-gather.3.cloned.1.call-done, bf16[2,1536,768]{2,1,0:T(8,128)(2,1)} %param.16), kind=kOutput, calls=%fused_computation.33 | convolution fusion | flops 3028746240 | bytes 14548992 | tf_op jit(solution)/shard_map/abjcd,jdf->abjcf/dot_general | solution.py:133
  231.9 5.7 %fusion.30 = bf16[8,16,2,5,1536]{4,1,3,0,2:T(8,128)(2,1)S(1)} fusion(bf16[8,16,2,5,768]{4,1,3,0,2:T(8,128)(2,1)S(1)} %get-tuple-element.11, bf16[2,768,1536]{2,1,0:T(8,128)(2,1)} %param.17), kind=kOutput, calls=%fused_computation.39 | convolution fusion | flops 3021864960 | bytes 10616832 | tf_op jit(solution)/shard_map/abjcf,jfd->abjcd/dot_general | solution.py:138
  237.7 5.2 copy.25
  242.9 10.8 %reshape_reshape.8 = bf16[8,245760]{1,0:T(8,128)(2,1)} reshape(bf16[8,16,2,5,1536]{4,3,2,1,0:T(8,128)(2,1)} %copy.25) | data formatting | bytes 7864320 | tf_op jit(solution)/shard_map/reshape;reshape | solution.py:44
  253.7 8.7 %pad_maximum_fusion = bf16[8,442368]{1,0:T(8,128)(2,1)} fusion(bf16[8,245760]{1,0:T(8,128)(2,1)} %reshape_reshape.8, bf16[8,196608]{1,0:T(8,128)(2,1)} %convert_element_type.109), kind=kLoop, calls=%fused_computation.6 | loop fusion | flops 14155776 | bytes 14155776 | tf_op jit(solution)/shard_map/concatenate | solution.py:44
  262.4 9.2 %reshape.106 = bf16[27648,128]{1,0:T(8,128)(2,1)} reshape(bf16[8,442368]{1,0:T(8,128)(2,1)} %pad_maximum_fusion) | data formatting | bytes 14155776 | tf_op jit(solution)/shard_map/reshape | solution.py:46
  271.6 9.9 %fusion.20 = bf16[8,16,2,5,768]{4,1,3,0,2:T(8,128)(2,1)S(1)} fusion(f32[2,8,16,5,768]{4,2,3,1,0:T(8,128)} %get-tuple-element.12, bf16[8,16,2,5,1536]{4,1,3,0,2:T(8,128)(2,1)} %all-gather.5.cloned.1.call-done, bf16[2,768,1536]{2,1,0:T(8,128)(2,1)} %param.17), kind=kOutput, calls=%fused_computation.26 | convolution fusion | flops 3039559680 | bytes 14548992 | tf_op jit(solution)/shard_map/abjcd,jfd->abjcf/dot_general | solution.py:152
  285.2 5.3 %copy.31 = bf16[8,16,2,5,1536]{4,3,2,1,0:T(8,128)(2,1)} copy(bf16[8,16,2,5,1536]{4,1,3,0,2:T(8,128)(2,1)S(1)} %fusion.27) | data formatting | bytes 7864320 | tf_op jit(solution)/shard_map/convert_element_type | solution.py:120
  290.5 10.8 %reshape_reshape.9 = bf16[8,245760]{1,0:T(8,128)(2,1)} reshape(bf16[8,16,2,5,1536]{4,3,2,1,0:T(8,128)(2,1)} %copy.31) | data formatting | bytes 7864320 | tf_op jit(solution)/shard_map/reshape;reshape | solution.py:44
  301.4 8.5 %pad_maximum_fusion.1 = bf16[8,442368]{1,0:T(8,128)(2,1)} fusion(bf16[8,245760]{1,0:T(8,128)(2,1)} %reshape_reshape.9, bf16[8,196608]{1,0:T(8,128)(2,1)} %convert_element_type.119), kind=kLoop, calls=%fused_computation.7 | loop fusion | flops 14155776 | bytes 14155776 | tf_op jit(solution)/shard_map/concatenate | solution.py:44
  309.9 9.2 %reshape.110 = bf16[27648,128]{1,0:T(8,128)(2,1)} reshape(bf16[8,442368]{1,0:T(8,128)(2,1)} %pad_maximum_fusion.1) | data formatting | bytes 14155776 | tf_op jit(solution)/shard_map/reshape | solution.py:46
  319.1 109.3 %all-reduce.4.cloned.1.call-done = bf16[1179648]{0:T(1024)(128)(2,1)} async-done(((bf16[1179648]{0:T(1024)(128)(2,1)}), bf16[1179648]{0:T(1024)(128)(2,1)}) %all-reduce.4.cloned.1.call-update) | async-done | bytes 2359312 | tf_op jit(solution)/shard_map/psum | solution.py:57
  433.8 9.0 %bitcast_convert_fusion = bf16[2,768,1536]{2,1,0:T(8,128)(2,1)} fusion(bf16[8,16,2,5,1536]{4,1,3,0,2:T(8,128)(2,1)} %all-gather.5.cloned.1.call-done, bf16[8,16,2,5,768]{4,1,3,0,2:T(8,128)(2,1)} %copy-done.19), kind=kOutput, calls=%fused_computation.4 | convolution fusion | flops 3022258176 | bytes 10616832 | tf_op jit(solution)/shard_map/abjcf,abjcd->jfd/dot_general | solution.py:156
  442.8 5.8 %bitcast_convert_fusion.1 = bf16[2,1536,768]{2,1,0:T(8,128)(2,1)} fusion(bf16[8,16,2,5,1536]{4,1,3,0,2:T(8,128)(2,1)S(1)} %copy-done.14, bf16[8,16,2,5,768]{4,1,3,0,2:T(8,128)(2,1)S(1)} %copy-done.21), kind=kOutput, calls=%fused_computation.5 | convolution fusion | flops 3022258176 | bytes 10616832 | tf_op jit(solution)/shard_map/abjcd,abjcf->jdf/dot_general | solution.py:159
  451.7 10.7 %all-to-all-start.3 = ((bf16[16,2,5,1536]{3,1,2,0:T(2,128)(2,1)}), bf16[16,2,5,1536]{3,1,2,0:T(2,128)(2,1)S(1)}, u32[]{:S(2)}, u32[]{:S(2)}) async-start(bf16[16,2,5,1536]{3,1,2,0:T(2,128)(2,1)} %copy.26), calls=%async_computation.4 | async-start | bytes 983040 | tf_op jit(solution)/shard_map/all_to_all | solution.py:126
  462.4 24.1 %reduce-scatter.5.cloned.1.call-done = bf16[3456,128]{1,0:T(8,128)(2,1)} async-done(((bf16[27648,128]{1,0:T(8,128)(2,1)}), bf16[3456,128]{1,0:T(8,128)(2,1)}) %reduce-scatter.5.cloned.1.call-update) | async-done | bytes 884752 | tf_op jit(solution)/shard_map/reduce_scatter | solution.py:47
  493.1 7.1 %all-to-all-start.7 = ((bf16[16,2,5,1536]{3,1,2,0:T(2,128)(2,1)}), bf16[16,2,5,1536]{3,1,2,0:T(2,128)(2,1)}, u32[]{:S(2)}, u32[]{:S(2)}) async-start(bf16[16,2,5,1536]{3,1,2,0:T(2,128)(2,1)} %copy.32), calls=%async_computation.9 | async-start | bytes 983040 | tf_op jit(solution)/shard_map/all_to_all | solution.py:126
  506.0 5.2 %all-to-all-done.7 = bf16[16,2,5,1536]{3,1,2,0:T(2,128)(2,1)} async-done(((bf16[16,2,5,1536]{3,1,2,0:T(2,128)(2,1)}), bf16[16,2,5,1536]{3,1,2,0:T(2,128)(2,1)}, u32[]{:S(2)}, u32[]{:S(2)}) %all-to-all-start.7) | async-done | bytes 491552 | tf_op jit(solution)/shard_map/all_to_all | solution.py:126
  (119 shorter events, 86.3 us)
Async XLA Ops:
  8.0 171.1 %copy-start = (bf16[1536,384]{1,0:T(8,128)(2,1)S(1)}, bf16[1536,384]{1,0:T(8,128)(2,1)}, u32[]{:S(2)}) copy-start(bf16[1536,384]{1,0:T(8,128)(2,1)} %param.18) | copy-start | bytes 3538948
  8.0 213.5 %all-gather.3.cloned.1.call-start = ((), (), s32[]{:S(2)}) async-start(), calls=%async_computation.10 | async-start | bytes 4423680 | tf_op jit(solution)/shard_map/all_gather | solution.py:111
  10.9 24.6 %copy-start.9 = (s32[128]{0:T(128)S(1)}, s32[128]{0:T(128)}, u32[]{:S(2)}) copy-start(s32[128]{0:T(128)} %param.13) | copy-start | bytes 1540
  10.9 24.6 %copy-start.11 = (s32[128]{0:T(128)S(1)}, s32[128]{0:T(128)}, u32[]{:S(2)}) copy-start(s32[128]{0:T(128)} %param.14) | copy-start | bytes 1540
  10.9 24.6 %copy-start.13 = (f32[128]{0:T(128)S(1)}, f32[128]{0:T(128)}, u32[]{:S(2)}) copy-start(f32[128]{0:T(128)} %param.11) | copy-start | bytes 1540
  10.9 24.6 %copy-start.2 = (bf16[128,1536]{1,0:T(8,128)(2,1)S(1)}, bf16[128,1536]{1,0:T(8,128)(2,1)}, u32[]{:S(2)}) copy-start(bf16[128,1536]{1,0:T(8,128)(2,1)} %param.15) | copy-start | bytes 1179652
  63.0 59.4 %copy-start.6 = (bf16[128,1536]{1,0:T(8,128)(2,1)S(1)}, bf16[128,1536]{1,0:T(8,128)(2,1)}, u32[]{:S(2)}) copy-start(bf16[128,1536]{1,0:T(8,128)(2,1)} %param.10) | copy-start | bytes 1179652
  124.4 54.7 %all-to-all-start = ((bf16[8,128,1536]{2,1,0:T(8,128)(2,1)}), bf16[8,128,1536]{2,1,0:T(8,128)(2,1)}, u32[]{:S(2)}, u32[]{:S(2)}) async-start(bf16[8,128,1536]{2,1,0:T(8,128)(2,1)} %stack.4), calls=%async_computation | async-start | bytes 6291456 | tf_op jit(solution)/shard_map/all_to_all | solution.py:13
  128.8 142.7 %all-gather.5.cloned.1.call-start = ((), (), s32[]{:S(2)}) async-start(), calls=%async_computation.12 | async-start | bytes 4423680 | tf_op jit(solution)/shard_map/all_gather | solution.py:111
  130.4 298.1 %all-reduce.4.cloned.1.call-start = ((), (), s32[]{:S(2)}) async-start(), calls=%async_computation.14 | async-start | bytes 4718592 | tf_op jit(solution)/shard_map/psum | solution.py:57
  179.1 4.7 copy-start.4
  207.7 5.1 copy-start.15
  207.7 5.1 copy-start.18
  221.3 227.4 %reduce-scatter.3.cloned.1.call-start = ((), (), s32[]{:S(2)}) async-start(), calls=%async_computation.11 | async-start | bytes 7962624 | tf_op jit(solution)/shard_map/reduce_scatter | solution.py:47
  262.4 19.1 %slice-start.1 = ((s8[4718592]{0:T(1024)(128)(4,1)}), s8[524288]{0:T(1024)(128)(4,1)S(1)}, s32[]{:S(2)}) async-start(s8[4718592]{0:T(1024)(128)(4,1)} %bitcast.90), calls=%async_computation.16 | async-start | bytes 1048576
  271.6 9.9 %slice-start.2 = ((s8[4718592]{0:T(1024)(128)(4,1)}), s8[4194304]{0:T(1024)(128)(4,1)S(1)}, s32[]{:S(2)}) async-start(s8[4718592]{0:T(1024)(128)(4,1)} %bitcast.90), calls=%async_computation.17 | async-start | bytes 8388608
  281.5 3.7 copy-start.20
  301.3 185.1 %reduce-scatter.5.cloned.1.call-start = ((), (), s32[]{:S(2)}) async-start(), calls=%async_computation.13 | async-start | bytes 7962624 | tf_op jit(solution)/shard_map/reduce_scatter | solution.py:47
  433.8 9.0 %copy-start.14 = (bf16[8,16,2,5,1536]{4,1,3,0,2:T(8,128)(2,1)S(1)}, bf16[8,16,2,5,1536]{4,1,3,0,2:T(8,128)(2,1)}, u32[]{:S(2)}) copy-start(bf16[8,16,2,5,1536]{4,1,3,0,2:T(8,128)(2,1)} %all-gather.3.cloned.1.call-done) | copy-start | bytes 11796484
  433.8 9.0 %copy-start.21 = (bf16[8,16,2,5,768]{4,1,3,0,2:T(8,128)(2,1)S(1)}, bf16[8,16,2,5,768]{4,1,3,0,2:T(8,128)(2,1)}, u32[]{:S(2)}) copy-start(bf16[8,16,2,5,768]{4,1,3,0,2:T(8,128)(2,1)} %copy-done.20) | copy-start | bytes 5898244
  451.7 40.6 %all-to-all-start.3 = ((bf16[16,2,5,1536]{3,1,2,0:T(2,128)(2,1)}), bf16[16,2,5,1536]{3,1,2,0:T(2,128)(2,1)S(1)}, u32[]{:S(2)}, u32[]{:S(2)}) async-start(bf16[16,2,5,1536]{3,1,2,0:T(2,128)(2,1)} %copy.26), calls=%async_computation.4 | async-start | bytes 983040 | tf_op jit(solution)/shard_map/all_to_all | solution.py:126
  493.1 18.1 %all-to-all-start.7 = ((bf16[16,2,5,1536]{3,1,2,0:T(2,128)(2,1)}), bf16[16,2,5,1536]{3,1,2,0:T(2,128)(2,1)}, u32[]{:S(2)}, u32[]{:S(2)}) async-start(bf16[16,2,5,1536]{3,1,2,0:T(2,128)(2,1)} %copy.32), calls=%async_computation.9 | async-start | bytes 983040 | tf_op jit(solution)/shard_map/all_to_all | solution.py:126
  501.4 3.2 copy-start.3
  501.4 3.1 copy-start.8
  (9 other events, 18.2 us)
Sparse Core Ops, SparseCore 0:
  35.6 82.5 all-gather.2
  131.3 74.7 all-gather.4
  301.5 95.7 reduce-scatter.2
  399.5 86.9 reduce-scatter.4
Sparse Core Ops, SparseCore 1:
  221.3 207.1 all-reduce.3
